TPU v7x, 128 devices: a whole 4x4x4 slice. The times are simulated.
128 devices in a mesh: rep: 16 (over x, y_lo, core), tp: 8 (over z, y_hi).
Axes of the slice: x: 4, y: 4 (y_hi: 2, y_lo: 2; y = y_hi * 2 + y_lo), z: 4, core: 2. Of those that a mesh axis runs over, the one named last changes fastest.
Arguments:
- context: bfloat16 [32768, 5120], P('rep', 'tp'), may hold values from -6 to 6
- out_grad: bfloat16 [32768, 5120], P('rep', 'tp'), may hold values from -6 to 6
- rewards: int32 [8, 64], P(None, 'rep'), may hold values from 0 to 1
- master: float32 [5120, 5120], P('rep', 'tp'), may hold values from -0.078125 to 0.078125
- first_moment: float32 [5120, 5120], P('rep', 'tp'), may hold values from -0.03125 to 0.03125
- second_moment: float32 [5120, 5120], P('rep', 'tp'), may hold values from 3.0517577e-07 to 3.0517578e-05
- inputs: bfloat16 [4, 512, 5120], P(None, 'rep'), may hold values from -6 to 6
- w_query: bfloat16 [5120, 5120], P(None, 'tp'), may hold values from -0.078125 to 0.078125
- w_key: bfloat16 [5120, 1024], P(None, 'tp'), may hold values from -0.078125 to 0.078125
- w_value: bfloat16 [5120, 1024], P(None, 'tp'), may hold values from -0.078125 to 0.078125
- cache_keys: bfloat16 [512, 256, 1024], P('rep', None, 'tp'), may hold values from -400 to 400
- cache_values: bfloat16 [512, 256, 1024], P('rep', None, 'tp'), may hold values from -24 to 24
- lengths: int32 [64], P('rep'), may hold values from 64 to 256
Outputs:
- decoded: bfloat16 [4, 512, 5120], P(None, 'rep')
- adam_step: float32 [5120, 5120], P('rep', 'tp')
All inputs are finite; a program needn't handle non-finite values.
Results may differ from a plain program's by a relative error of at most 0.0088.
Values may be sent and summed in bfloat16 or wider, within the bound.
A program may use at most 128 MiB of HBM per device.

v0:
```python
import jax
import jax.numpy as jnp
from jax import lax
from jax.sharding import PartitionSpec as P

HEAD_DIM = 128
rope_base = 1000000.0
first_beta = 0.9
second_beta = 0.95
adam_epsilon = 1e-08
step_count = 10
learn_rate = 0.001


def from_everyone(array, axis):
    devices = lax.axis_size(axis)
    return lax.all_to_all(
        jnp.broadcast_to(array[None], (devices, *array.shape)), axis, 0, 0, tiled=True
    )


def of_everyone(array, axis):
    everything = from_everyone(array, axis)
    return jnp.sum(everything, axis=0)


def laid_out(tiles, dim):
    tiles = jnp.moveaxis(tiles, 0, dim)
    lengths = tiles.shape
    return tiles.reshape(*lengths[:dim], lengths[dim] * lengths[dim + 1], *lengths[dim + 2 :])


def collect(array, axis, dim):
    return laid_out(from_everyone(array, axis), dim)


def split_up(array, dim, devices):
    before, after = (array.shape[:dim], array.shape[dim + 1 :])
    return jnp.moveaxis(array.reshape(*before, devices, -1, *after), dim, 0)


def sum_at_owner(array, axis, dim):
    tiles = split_up(array, dim, lax.axis_size(axis))
    arrived = lax.all_to_all(tiles, axis, split_axis=0, concat_axis=0, tiled=True)
    return arrived.sum(axis=0)


def rotate(vectors, positions):
    half_dim = vectors.shape[-1] // 2
    frequency = rope_base ** (-2.0 * jnp.arange(half_dim, dtype=jnp.float32) / vectors.shape[-1])
    angles = positions[..., None].astype(jnp.float32) * frequency
    cosine_table = jnp.cos(angles)
    sine_table = jnp.sin(angles)
    former = vectors[..., :half_dim]
    latter = vectors[..., half_dim:]
    return jnp.concatenate(
        [former * cosine_table - latter * sine_table, latter * cosine_table + former * sine_table],
        axis=-1,
    )


def attend(queries, old_keys, old_values, new_keys, new_values, live_mask):
    score_scale = HEAD_DIM ** (-0.5)
    step_total = queries.shape[0]
    cache_scores = (
        jnp.einsum("tsgqd,scgd->tsgqc", queries, old_keys, preferred_element_type=jnp.float32)
        * score_scale
    )
    cache_scores = jnp.where(live_mask[None, :, None, None, :], cache_scores, -1e30)
    recent = (
        jnp.einsum("tsgqd,usgd->tsgqu", queries, new_keys, preferred_element_type=jnp.float32)
        * score_scale
    )
    causal = jnp.arange(step_total)[:, None] >= jnp.arange(step_total)[None, :]
    recent = jnp.where(causal[:, None, None, None, :], recent, -1e30)
    row_peak = jnp.maximum(jnp.max(cache_scores, axis=-1), jnp.max(recent, axis=-1))[..., None]
    cache_exp = jnp.exp(cache_scores - row_peak)
    recent_exp = jnp.exp(recent - row_peak)
    denominator = jnp.sum(cache_exp, axis=-1, keepdims=True) + jnp.sum(
        recent_exp, axis=-1, keepdims=True
    )
    cache_weight = (cache_exp / denominator).astype(jnp.bfloat16)
    recent_weight = (recent_exp / denominator).astype(jnp.bfloat16)
    attended = jnp.einsum(
        "tsgqc,scgd->tsgqd", cache_weight, old_values, preferred_element_type=jnp.float32
    )
    attended = attended + jnp.einsum(
        "tsgqu,usgd->tsgqd", recent_weight, new_values, preferred_element_type=jnp.float32
    )
    return attended.astype(jnp.bfloat16)


def per_device(
    context,
    out_grad,
    rewards,
    master,
    first_moment,
    second_moment,
    inputs,
    w_query,
    w_key,
    w_value,
    cache_keys,
    cache_values,
    lengths,
):
    replicas = lax.axis_size("rep")
    prompt_count, local_group = rewards.shape
    totals = of_everyone(jnp.sum(rewards, axis=1), "rep")
    group_size = local_group * replicas
    advantage = rewards.astype(jnp.float32) - totals.astype(jnp.float32)[:, None] / group_size
    token_local = context.shape[0]
    per_token = jnp.repeat(advantage.reshape(-1), token_local // (prompt_count * local_group)) / (
        token_local * replicas
    )
    scaled = (out_grad.astype(jnp.float32) * per_token[:, None]).astype(jnp.bfloat16)
    features = lax.all_gather(context, "tp", axis=1, tiled=True)
    gradient = lax.psum_scatter(
        lax.dot_general(
            features, scaled, (((0,), (0,)), ((), ())), preferred_element_type=jnp.float32
        ).astype(jnp.bfloat16),
        "rep",
        scatter_dimension=0,
        tiled=True,
    ).astype(jnp.float32)
    moment_new = first_beta * first_moment + (1.0 - first_beta) * gradient
    square_new = second_beta * second_moment + (1.0 - second_beta) * gradient * gradient
    adam_step = (
        moment_new
        / (1.0 - first_beta**step_count)
        / (jnp.sqrt(square_new / (1.0 - second_beta**step_count)) + adam_epsilon)
    )
    weight = (master - learn_rate * adam_step).astype(jnp.bfloat16)
    step_total, seq_local, model_width = inputs.shape
    local_heads = w_query.shape[1] // HEAD_DIM
    local_kv = w_key.shape[1] // HEAD_DIM
    flat_rows = inputs.reshape(step_total * seq_local, model_width)
    queries = jnp.dot(flat_rows, w_query, preferred_element_type=jnp.float32).reshape(
        step_total, seq_local, local_heads, HEAD_DIM
    )
    key_new = jnp.dot(flat_rows, w_key, preferred_element_type=jnp.float32).reshape(
        step_total, seq_local, local_kv, HEAD_DIM
    )
    value_new = (
        jnp.dot(flat_rows, w_value, preferred_element_type=jnp.float32)
        .reshape(step_total, seq_local, local_kv, HEAD_DIM)
        .astype(jnp.bfloat16)
    )
    seq_length = jnp.repeat(lengths, seq_local // lengths.shape[0])
    positions = seq_length[None, :] + jnp.arange(step_total, dtype=jnp.int32)[:, None]
    queries = rotate(queries, positions[:, :, None]).astype(jnp.bfloat16)
    queries = queries.reshape(step_total, seq_local, local_kv, local_heads // local_kv, HEAD_DIM)
    key_new = rotate(key_new, positions[:, :, None]).astype(jnp.bfloat16)
    slot_total = cache_keys.shape[1]
    old_keys = cache_keys.reshape(seq_local, slot_total, local_kv, HEAD_DIM)
    old_values = cache_values.reshape(seq_local, slot_total, local_kv, HEAD_DIM)
    live_mask = jnp.arange(slot_total, dtype=jnp.int32)[None, :] < seq_length[:, None]
    attended = attend(queries, old_keys, old_values, key_new, value_new, live_mask)
    attended = attended.reshape(step_total * seq_local, local_heads * HEAD_DIM)
    all_heads = collect(attended, "tp", 1)
    feature_rows = lax.all_to_all(all_heads, "rep", split_axis=1, concat_axis=0, tiled=True)
    own_columns = sum_at_owner(
        jnp.dot(feature_rows, weight, preferred_element_type=jnp.float32), "rep", 0
    )
    decoded = collect(own_columns.astype(jnp.bfloat16), "tp", 1)
    return (decoded.reshape(step_total, seq_local, model_width), adam_step)


def solution(mesh):
    placed = (
        P("rep", "tp"),
        P("rep", "tp"),
        P(None, "rep"),
        P("rep", "tp"),
        P("rep", "tp"),
        P("rep", "tp"),
        P(None, "rep", None),
        P(None, "tp"),
        P(None, "tp"),
        P(None, "tp"),
        P("rep", None, "tp"),
        P("rep", None, "tp"),
        P("rep"),
    )
    return jax.shard_map(
        per_device,
        mesh=mesh,
        in_specs=placed,
        out_specs=(P(None, "rep", None), P("rep", "tp")),
        check_vma=False,
    )
```

profile of v0, /device:TPU:0, one launch (start us, length us, event | category | flops | bytes accessed | tf_op | source)
XLA Modules:
  0.0 483.4 jit_solution(15974922212269263185)
XLA Ops:
  7.2 0.7 all-gather.2.cloned.1.call-update
  8.0 11.4 %all_to_all.37 = s32[16,1,8]{2,1,0:T(1,128)S(1)} all-to-all(s32[16,1,8]{2,1,0:T(1,128)S(1)} %broadcast_in_dim.69), channel_id=1, replica_groups=mesh['rep'=16,'tp'=8] {'rep'}, dimensions={0} | all-to-all | bytes 1024 | tf_op jit(solution)/shard_map/all_to_all | solution.py:17
  19.5 0.1 copy.87
  19.6 0.1 div.61
  19.7 0.1 broadcast_in_dim.70
  19.7 0.1 div.62
  19.8 212.7 %all-gather.2.cloned.1.call-done = bf16[2048,5120]{1,0:T(8,128)(2,1)} async-done(((bf16[2048,640]{1,0:T(8,128)(2,1)}), bf16[2048,5120]{1,0:T(8,128)(2,1)}) %all-gather.2.cloned.1.call-update) | async-done | bytes 20971536 | tf_op jit(solution)/shard_map/all_gather | solution.py:118
  232.5 20.7 %fusion = bf16[5120,640]{0,1:T(8,128)(2,1)} fusion(bf16[2048,5120]{1,0:T(8,128)(2,1)} %all-gather.2.cloned.1.call-done, bf16[2048,640]{1,0:T(8,128)(2,1)} %param.14, f32[2048]{0:T(1024)S(1)} %div.62), kind=kOutput, calls=%fused_computation.1 | convolution fusion | flops 13428981760 | bytes 30154752 | tf_op jit(solution)/shard_map/dot_general | solution.py:120
  253.2 9.5 %copy.104 = bf16[5120,640]{1,0:T(8,128)(2,1)} copy(bf16[5120,640]{0,1:T(8,128)(2,1)} %fusion) | data formatting | bytes 13107200
  262.7 0.6 copy-done.6
  263.4 0.1 broadcast_in_dim.36
  263.4 0.1 lt.20
  263.5 9.7 %copy.78 = bf16[5120,640]{0,1:T(8,128)(2,1)} copy(bf16[5120,640]{1,0:T(8,128)(2,1)} %param.20) | data formatting | bytes 13107200 | tf_op args[7]
  273.3 1.8 fusion.32
  275.1 0.3 fusion.71
  275.4 0.1 maximum_bitcast_fusion
  275.5 0.3 multiply_cosine_fusion.1
  275.8 5.1 %fusion.12 = f32[4,32,5,128]{3,1,2,0:T(8,128)S(1)} fusion(bf16[5,128,5120,1]{2,1,0,3:T(8,128)(2,1)} %bitcast.105, bf16[4,32,5120]{2,1,0:T(8,128)(2,1)S(1)} %copy-done.1), kind=kOutput, calls=%fused_computation.11 | convolution fusion | flops 838860800 | bytes 8192000 | tf_op jit(solution)/shard_map/dot_general | solution.py:139
  280.9 0.2 subtract_convert_fusion.1
  281.1 0.1 pad_maximum_fusion
  281.2 0.1 iota_compare_fusion
  281.3 1.3 fusion.74
  282.7 0.8 fusion.73
  283.5 0.3 fusion.57
  283.8 0.5 fusion.49
  284.3 0.5 fusion.38
  284.8 0.7 copy-done.7
  285.4 0.6 fusion.26
  286.1 0.4 fusion.30
  286.5 0.2 copy.84
  286.7 0.2 broadcast_in_dim.68
  286.9 38.0 %all_to_all.38 = bf16[8,128,640]{1,2,0:T(8,128)(2,1)} all-to-all(bf16[8,128,640]{1,2,0:T(8,128)(2,1)S(1)} %broadcast_in_dim.68), channel_id=1, replica_groups=mesh['rep'=16,'tp'=8] {'tp'}, dimensions={0} | all-to-all | bytes 2621440 | tf_op jit(solution)/shard_map/all_to_all | solution.py:17
  324.9 6.1 %all-to-all-start.1 = ((bf16[128,16,320]{0,2,1:T(8,128)(2,1)}), bf16[128,16,320]{0,2,1:T(8,128)(2,1)}, u32[]{:S(2)}, u32[]{:S(2)}) async-start(bf16[128,16,320]{0,2,1:T(8,128)(2,1)} %bitcast.27), calls=%async_computation.1 | async-start | bytes 2621440 | tf_op jit(solution)/shard_map/all_to_all | solution.py:162
  331.0 1.3 copy.89
  332.3 2.5 copy.85
  334.9 1.3 copy.88
  336.1 33.8 %reduce-scatter.4.cloned.1.call-done = bf16[320,640]{1,0:T(8,128)(2,1)} async-done(((bf16[5120,640]{1,0:T(8,128)(2,1)}), bf16[320,640]{1,0:T(8,128)(2,1)}) %reduce-scatter.4.cloned.1.call-update) | async-done | bytes 409616
  370.0 2.0 copy.105
  371.9 2.3 fusion.44
  374.2 3.4 fusion.14
  377.6 67.4 %all_to_all.39 = f32[16,128,640]{2,1,0:T(8,128)} all-to-all(f32[16,128,640]{2,1,0:T(8,128)S(1)} %fusion.14), channel_id=1, replica_groups=mesh['rep'=16,'tp'=8] {'rep'}, dimensions={0} | all-to-all | bytes 10485760 | tf_op jit(solution)/shard_map/all_to_all | solution.py:44
  445.0 2.7 reduce_sum.49
  447.8 1.2 broadcast_in_dim.71
  448.9 4.3 all-to-all-start.4
  453.2 1.2 copy.92
  454.4 18.6 %all-to-all-done.4 = bf16[8,128,640]{2,1,0:T(8,128)(2,1)} async-done(((bf16[8,128,640]{2,1,0:T(8,128)(2,1)}), bf16[8,128,640]{2,1,0:T(8,128)(2,1)}, u32[]{:S(2)}, u32[]{:S(2)}) %all-to-all-start.4) | async-done | bytes 1310752 | tf_op jit(solution)/shard_map/all_to_all | solution.py:17
  473.0 2.1 copy.91
  475.1 1.5 reshape_reshape.3
  (30 shorter events, 0.4 us)
Async XLA Ops:
  7.2 275.5 %copy-start = (bf16[32,256,128]{2,1,0:T(8,128)(2,1)S(1)}, bf16[32,256,128]{2,1,0:T(8,128)(2,1)}, u32[]{:S(2)}) copy-start(bf16[32,256,128]{2,1,0:T(8,128)(2,1)} %param.23) | copy-start | bytes 6291460
  7.2 0.8 copy-start.5
  7.2 225.3 %all-gather.2.cloned.1.call-start = ((), (), s32[]{:S(2)}) async-start(), calls=%async_computation.6 | async-start | bytes 23592960 | tf_op jit(solution)/shard_map/all_gather | solution.py:118
  7.9 362.0 %reduce-scatter.4.cloned.1.call-start = ((), (), s32[]{:S(2)}) async-start(), calls=%async_computation.7 | async-start | bytes 6963200
  262.7 0.7 copy-start.6
  263.5 9.8 %copy-start.1 = (bf16[4,32,5120]{2,1,0:T(8,128)(2,1)S(1)}, bf16[4,32,5120]{2,1,0:T(8,128)(2,1)}, u32[]{:S(2)}) copy-start(bf16[4,32,5120]{2,1,0:T(8,128)(2,1)} %param.19) | copy-start | bytes 3932164
  282.6 1.6 copy-start.2
  283.8 1.7 copy-start.7
  286.9 44.2 %copy-start.3 = (f32[320,640]{1,0:T(8,128)S(1)}, f32[320,640]{1,0:T(8,128)}, u32[]{:S(2)}) copy-start(f32[320,640]{1,0:T(8,128)} %param.16) | copy-start | bytes 2457604
  324.9 49.3 %all-to-all-start.1 = ((bf16[128,16,320]{0,2,1:T(8,128)(2,1)}), bf16[128,16,320]{0,2,1:T(8,128)(2,1)}, u32[]{:S(2)}, u32[]{:S(2)}) async-start(bf16[128,16,320]{0,2,1:T(8,128)(2,1)} %bitcast.27), calls=%async_computation.1 | async-start | bytes 2621440 | tf_op jit(solution)/shard_map/all_to_all | solution.py:162
  332.3 2.5 copy-start.4
  448.9 24.1 %all-to-all-start.4 = ((bf16[8,128,640]{2,1,0:T(8,128)(2,1)}), bf16[8,128,640]{2,1,0:T(8,128)(2,1)}, u32[]{:S(2)}, u32[]{:S(2)}) async-start(bf16[8,128,640]{2,1,0:T(8,128)(2,1)} %broadcast_in_dim.71), calls=%async_computation.4 | async-start | bytes 2621440 | tf_op jit(solution)/shard_map/all_to_all | solution.py:17
Sparse Core Ops, SparseCore 0:
  10.4 222.0 all-gather.1
  262.9 107.0 reduce-scatter.3
where the time goes:
time: 484 us; the launch traced here: 483 us
  waiting for transfers between devices  266 us (55%)
  blocking collectives  117 us (24%)
  matrix products  34.6 us (7%)
  local copies, waits for them, and re-layouts  34.5 us (7%)
  between operations  14.3 us (3%)
  starting transfers between devices  10.4 us (2%)
  other arithmetic  6.95 us (1%)
    all_gather x1, waiting for transfers between devices, per_device(): features = lax.all_gather(context, 'tp', axis=1, tiled=True)  213 us
    all_to_all x1, blocking collectives, sum_at_owner(): lax.all_to_all(tiles, axis, split_axis=0, concat_axis=0, tiled=True)  67.4 us
    all_to_all x2, blocking collectives, from_everyone(): lax.all_to_all(jnp.broadcast_to(array[None], (devices, *array.shape)), ax...  49.5 us
    unnamed x3, waiting for transfers between devices  34.5 us
    unnamed x24, local copies, waits for them, and re-layouts  28.9 us
    dot_general x1, matrix products, per_device(): lax.dot_general(features, scaled, (((0,), (0,)), ((), ())), preferred_ele...  20.7 us
    all_to_all x1, waiting for transfers between devices, from_everyone(): lax.all_to_all(jnp.broadcast_to(array[None], (devices, *array.shape)), ax...  18.6 us
  transfers between devices with their start and end apart: 4, of which 3 were waited for; matrix products, arithmetic and copies ran while one was open for 7% of the time, Pallas kernels for 0%

commit v1 on v0

--- a/solution.py
+++ b/solution.py
@@ -115,7 +115,9 @@
         token_local * replicas
     )
     scaled = (out_grad.astype(jnp.float32) * per_token[:, None]).astype(jnp.bfloat16)
-    features = lax.all_gather(context, "tp", axis=1, tiled=True)
+    features = jnp.concatenate(
+        lax.all_to_all(jnp.stack([context] * lax.axis_size("tp")), "tp", 0, 0), axis=1
+    )
     gradient = lax.psum_scatter(
         lax.dot_general(
             features, scaled, (((0,), (0,)), ((), ())), preferred_element_type=jnp.float32

time: 484 us -> 519 us (1.072)
  waiting for transfers between devices: 266 us -> 283 us
  starting transfers between devices: 10.4 us -> 25.2 us
  local copies, waits for them, and re-layouts: 34.5 us -> 47.8 us
  blocking collectives: 117 us -> 105 us
    all_to_all x0 -> x1, waiting for transfers between devices: none -> 230 us  [per_device(): lax.all_to_all(jnp.stack([context] * lax.axis_size('tp')), 'tp', 0, 0)]
    all_gather x1 -> x0, waiting for transfers between devices: 213 us -> none  [per_device(): features = lax.all_gather(context, 'tp', axis=1, tiled=True)]
    all_to_all x2 -> x1, blocking collectives: 49.5 us -> 37.9 us  [from_everyone(): lax.all_to_all(jnp.broadcast_to(array[None], (devices, *array.shape)), ax...]
    another operation x0 -> x1, local copies, waits for them, and re-layouts: none -> 8.39 us  [per_device(): jnp.stack([context] * lax.axis_size('tp'))]
    all_to_all x0 -> x1, starting transfers between devices: none -> 7.78 us  [per_device(): lax.all_to_all(jnp.stack([context] * lax.axis_size('tp')), 'tp', 0, 0)]
    all_to_all x1 -> x2, starting transfers between devices: 4.26 us -> 11.5 us  [from_everyone(): lax.all_to_all(jnp.broadcast_to(array[None], (devices, *array.shape)), ax...]
    unnamed x24 -> x25, local copies, waits for them, and re-layouts: 28.9 us -> 33.3 us
    unnamed x3 -> x2, waiting for transfers between devices: 34.5 us -> 32.5 us
  transfers between devices with their start and end apart: 4 -> 5, of which waited for: 3 -> 4; matrix products, arithmetic and copies ran while one was open for 7% -> 7% of each run, Pallas kernels for 0% -> 0%
where the time goes in v1:
time: 519 us; the launch traced here: 518 us
  waiting for transfers between devices  283 us (55%)
  blocking collectives  105 us (20%)
  local copies, waits for them, and re-layouts  47.8 us (9%)
  matrix products  35.1 us (7%)
  starting transfers between devices  25.2 us (5%)
  between operations  14.3 us (3%)
  other arithmetic  7.78 us (1%)
    all_to_all x1, waiting for transfers between devices, per_device(): lax.all_to_all(jnp.stack([context] * lax.axis_size('tp')), 'tp', 0, 0)  230 us
    all_to_all x1, blocking collectives, sum_at_owner(): lax.all_to_all(tiles, axis, split_axis=0, concat_axis=0, tiled=True)  67.3 us
    all_to_all x1, blocking collectives, from_everyone(): lax.all_to_all(jnp.broadcast_to(array[None], (devices, *array.shape)), ax...  37.9 us
    unnamed x25, local copies, waits for them, and re-layouts  33.3 us
    unnamed x2, waiting for transfers between devices  32.5 us
    dot_general x1, matrix products, per_device(): lax.dot_general(features, scaled, (((0,), (0,)), ((), ())), preferred_ele...  21.2 us
    all_to_all x2, waiting for transfers between devices, from_everyone(): lax.all_to_all(jnp.broadcast_to(array[None], (devices, *array.shape)), ax...  19.9 us
    all_to_all x2, starting transfers between devices, from_everyone(): lax.all_to_all(jnp.broadcast_to(array[None], (devices, *array.shape)), ax...  11.5 us
  transfers between devices with their start and end apart: 5, of which 4 were waited for; matrix products, arithmetic and copies ran while one was open for 7% of the time, Pallas kernels for 0%

profile of v1, /device:TPU:0, one launch (start us, length us, event | category | flops | bytes accessed | tf_op | source)
XLA Modules:
  0.0 518.0 jit_solution(10915479923971549798)
XLA Ops:
  7.2 0.8 reduce_sum.47
  8.0 0.6 broadcast_in_dim.69
  8.6 5.5 %all-to-all-start.2 = ((s32[16,1,8]{2,1,0:T(1,128)}), s32[16,1,8]{2,1,0:T(1,128)S(1)}, u32[]{:S(2)}, u32[]{:S(2)}) async-start(s32[16,1,8]{2,1,0:T(1,128)} %broadcast_in_dim.69), calls=%async_computation.2 | async-start | bytes 16384 | tf_op jit(solution)/shard_map/all_to_all | solution.py:17
  14.2 4.5 copy.92
  18.7 1.5 all-to-all-done.2
  20.2 8.4 %stack.2 = bf16[8,2048,640]{1,2,0:T(8,128)(2,1)} broadcast(bf16[2048,640]{0,1:T(8,128)(2,1)} %copy.92), dimensions={1,2} | broadcast | bytes 23592960 | tf_op jit(solution)/shard_map/stack | solution.py:119
  28.6 7.8 %all-to-all-start.3 = ((bf16[8,2048,640]{1,2,0:T(8,128)(2,1)}), bf16[8,2048,640]{1,2,0:T(8,128)(2,1)}, u32[]{:S(2)}, u32[]{:S(2)}) async-start(bf16[8,2048,640]{1,2,0:T(8,128)(2,1)} %stack.2), calls=%async_computation.3 | async-start | bytes 41943040 | tf_op jit(solution)/shard_map/all_to_all | solution.py:119
  36.5 0.1 copy.91
  36.8 230.4 %all-to-all-done.3 = bf16[8,2048,640]{1,2,0:T(8,128)(2,1)} async-done(((bf16[8,2048,640]{1,2,0:T(8,128)(2,1)}), bf16[8,2048,640]{1,2,0:T(8,128)(2,1)}, u32[]{:S(2)}, u32[]{:S(2)}) %all-to-all-start.3) | async-done | bytes 20971552 | tf_op jit(solution)/shard_map/all_to_all | solution.py:119
  267.2 21.2 %fusion = bf16[5120,640]{0,1:T(8,128)(2,1)} fusion(bf16[2048,5120]{0,1:T(8,128)(2,1)} %bitcast.30, bf16[2048,640]{1,0:T(8,128)(2,1)} %param.14, f32[2048]{0:T(1024)S(1)} %div.62), kind=kOutput, calls=%fused_computation.1 | convolution fusion | flops 13428981760 | bytes 30154752 | tf_op jit(solution)/shard_map/dot_general | solution.py:122
  288.4 9.5 %copy.109 = bf16[5120,640]{1,0:T(8,128)(2,1)} copy(bf16[5120,640]{0,1:T(8,128)(2,1)} %fusion) | data formatting | bytes 13107200
  297.9 0.6 copy-done.6
  298.6 0.1 lt.20
  298.7 9.7 %copy.82 = bf16[5120,640]{0,1:T(8,128)(2,1)} copy(bf16[5120,640]{1,0:T(8,128)(2,1)} %param.20) | data formatting | bytes 13107200 | tf_op args[7]
  308.4 1.8 fusion.32
  310.3 0.3 fusion.71
  310.6 0.1 maximum_bitcast_fusion
  310.7 0.3 multiply_cosine_fusion.1
  311.0 5.1 fusion.12
  316.1 0.2 subtract_convert_fusion.1
  316.3 0.1 pad_maximum_fusion
  316.5 1.3 fusion.74
  317.8 0.8 fusion.73
  318.6 0.3 fusion.57
  318.9 0.5 fusion.49
  319.4 0.5 fusion.38
  319.9 0.6 copy-done.7
  320.5 0.6 fusion.26
  321.2 0.4 fusion.30
  321.6 0.2 copy.88
  321.8 0.2 broadcast_in_dim.68
  322.0 37.9 %all_to_all.42 = bf16[8,128,640]{1,2,0:T(8,128)(2,1)} all-to-all(bf16[8,128,640]{1,2,0:T(8,128)(2,1)S(1)} %broadcast_in_dim.68), channel_id=1, replica_groups=mesh['rep'=16,'tp'=8] {'tp'}, dimensions={0} | all-to-all | bytes 2621440 | tf_op jit(solution)/shard_map/all_to_all | solution.py:17
  359.8 5.9 %all-to-all-start.1 = ((bf16[128,16,320]{0,2,1:T(8,128)(2,1)}), bf16[128,16,320]{0,2,1:T(8,128)(2,1)}, u32[]{:S(2)}, u32[]{:S(2)}) async-start(bf16[128,16,320]{0,2,1:T(8,128)(2,1)} %bitcast.27), calls=%async_computation.1 | async-start | bytes 2621440 | tf_op jit(solution)/shard_map/all_to_all | solution.py:164
  365.7 1.3 copy.89
  367.0 2.5 copy.93
  369.5 1.3 copy.94
  370.8 32.4 %reduce-scatter.4.cloned.1.call-done = bf16[320,640]{1,0:T(8,128)(2,1)} async-done(((bf16[5120,640]{1,0:T(8,128)(2,1)}), bf16[320,640]{1,0:T(8,128)(2,1)}) %reduce-scatter.4.cloned.1.call-update) | async-done | bytes 409616
  403.3 2.0 copy.110
  405.2 2.3 fusion.44
  407.5 3.4 fusion.14
  410.9 67.3 %all_to_all.43 = f32[16,128,640]{2,1,0:T(8,128)} all-to-all(f32[16,128,640]{2,1,0:T(8,128)S(1)} %fusion.14), channel_id=1, replica_groups=mesh['rep'=16,'tp'=8] {'rep'}, dimensions={0} | all-to-all | bytes 10485760 | tf_op jit(solution)/shard_map/all_to_all | solution.py:44
  478.2 2.7 reduce_sum.49
  480.9 1.2 broadcast_in_dim.71
  482.1 6.0 %all-to-all-start.5 = ((bf16[8,128,640]{2,1,0:T(8,128)(2,1)}), bf16[8,128,640]{2,1,0:T(8,128)(2,1)}, u32[]{:S(2)}, u32[]{:S(2)}) async-start(bf16[8,128,640]{2,1,0:T(8,128)(2,1)} %broadcast_in_dim.71), calls=%async_computation.5 | async-start | bytes 2621440 | tf_op jit(solution)/shard_map/all_to_all | solution.py:17
  488.1 1.2 copy.97
  489.3 18.4 %all-to-all-done.5 = bf16[8,128,640]{2,1,0:T(8,128)(2,1)} async-done(((bf16[8,128,640]{2,1,0:T(8,128)(2,1)}), bf16[8,128,640]{2,1,0:T(8,128)(2,1)}, u32[]{:S(2)}, u32[]{:S(2)}) %all-to-all-start.5) | async-done | bytes 1310752 | tf_op jit(solution)/shard_map/all_to_all | solution.py:17
  507.6 2.1 copy.96
  509.7 1.5 reshape_reshape.3
  (32 shorter events, 0.6 us)
Async XLA Ops:
  7.2 310.6 %copy-start = (bf16[32,256,128]{2,1,0:T(8,128)(2,1)S(1)}, bf16[32,256,128]{2,1,0:T(8,128)(2,1)}, u32[]{:S(2)}) copy-start(bf16[32,256,128]{2,1,0:T(8,128)(2,1)} %param.23) | copy-start | bytes 6291460
  8.6 11.5 %all-to-all-start.2 = ((s32[16,1,8]{2,1,0:T(1,128)}), s32[16,1,8]{2,1,0:T(1,128)S(1)}, u32[]{:S(2)}, u32[]{:S(2)}) async-start(s32[16,1,8]{2,1,0:T(1,128)} %broadcast_in_dim.69), calls=%async_computation.2 | async-start | bytes 16384 | tf_op jit(solution)/shard_map/all_to_all | solution.py:17
  28.6 7.9 %copy-start.5 = (s32[8,4]{0,1:T(4,128)S(1)}, s32[8,4]{0,1:T(4,128)}, u32[]{:S(2)}) copy-start(s32[8,4]{0,1:T(4,128)} %param.15) | copy-start | bytes 388
  28.6 238.6 %all-to-all-start.3 = ((bf16[8,2048,640]{1,2,0:T(8,128)(2,1)}), bf16[8,2048,640]{1,2,0:T(8,128)(2,1)}, u32[]{:S(2)}, u32[]{:S(2)}) async-start(bf16[8,2048,640]{1,2,0:T(8,128)(2,1)} %stack.2), calls=%async_computation.3 | async-start | bytes 41943040 | tf_op jit(solution)/shard_map/all_to_all | solution.py:119
  36.4 366.9 %reduce-scatter.4.cloned.1.call-start = ((), (), s32[]{:S(2)}) async-start(), calls=%async_computation.7 | async-start | bytes 6963200
  297.9 0.7 copy-start.6
  298.7 9.7 %copy-start.1 = (bf16[4,32,5120]{2,1,0:T(8,128)(2,1)S(1)}, bf16[4,32,5120]{2,1,0:T(8,128)(2,1)}, u32[]{:S(2)}) copy-start(bf16[4,32,5120]{2,1,0:T(8,128)(2,1)} %param.19) | copy-start | bytes 3932164
  317.8 1.6 copy-start.2
  318.9 1.7 copy-start.7
  321.9 43.7 %copy-start.3 = (f32[320,640]{1,0:T(8,128)S(1)}, f32[320,640]{1,0:T(8,128)}, u32[]{:S(2)}) copy-start(f32[320,640]{1,0:T(8,128)} %param.17) | copy-start | bytes 2457604
  359.8 47.7 %all-to-all-start.1 = ((bf16[128,16,320]{0,2,1:T(8,128)(2,1)}), bf16[128,16,320]{0,2,1:T(8,128)(2,1)}, u32[]{:S(2)}, u32[]{:S(2)}) async-start(bf16[128,16,320]{0,2,1:T(8,128)(2,1)} %bitcast.27), calls=%async_computation.1 | async-start | bytes 2621440 | tf_op jit(solution)/shard_map/all_to_all | solution.py:164
  367.0 2.5 copy-start.4
  482.1 25.6 %all-to-all-start.5 = ((bf16[8,128,640]{2,1,0:T(8,128)(2,1)}), bf16[8,128,640]{2,1,0:T(8,128)(2,1)}, u32[]{:S(2)}, u32[]{:S(2)}) async-start(bf16[8,128,640]{2,1,0:T(8,128)(2,1)} %broadcast_in_dim.71), calls=%async_computation.5 | async-start | bytes 2621440 | tf_op jit(solution)/shard_map/all_to_all | solution.py:17
Sparse Core Ops, SparseCore 0:
  298.0 105.2 reduce-scatter.3
